TPU v7x, 32 devices: a whole 2x2x4 slice. The times are simulated.
32 devices in a mesh: fsdp: 2 (over y), tensor: 16 (over z, x, core).
Axes of the slice: x: 2, y: 2, z: 4, core: 2. Of those that a mesh axis runs over, the one named last changes fastest.
Arguments:
- momentum: bfloat16 [8192, 28672], P('fsdp', 'tensor'), may hold values from -6 to 6
- gradient: bfloat16 [8192, 28672], P('fsdp', 'tensor'), may hold values from -4 to 4
- factor: float32 [28672, 512], P('tensor', 'fsdp'), may hold values from -0.03125 to 0.03125
Outputs:
- new_momentum: bfloat16 [8192, 28672], P('fsdp', 'tensor')
- new_factor: float32 [28672, 512], P('tensor', 'fsdp')
- update: bfloat16 [8192, 28672], P('fsdp', 'tensor')
All inputs are finite; a program needn't handle non-finite values.
Results may differ from a plain program's by a relative error of at most 0.017.
Values may be sent and summed in bfloat16 or wider, within the bound.
A program may use at most 128 MiB of HBM per device.

v0:
```python
import jax
import jax.numpy as jnp
from jax import lax
from jax.sharding import PartitionSpec as P

D = 8192
FF = 28672
R = 512


decay_rate = 0.95
epsilon = 1e-06


def on_device(momentum, gradient, factor):
    blended = (momentum.astype(jnp.float32) + gradient.astype(jnp.float32)).astype(jnp.bfloat16)
    lowered = factor.astype(jnp.bfloat16)
    partial_left = jnp.dot(
        blended,
        lax.all_gather(lowered, "fsdp", axis=1, tiled=True),
        preferred_element_type=jnp.float32,
    )
    left_factor = lax.psum(partial_left, "tensor")
    local_gram = lax.dot_general(
        left_factor, left_factor, (((0,), (0,)), ((), ())), precision=lax.Precision.HIGHEST
    )
    gram_matrix = lax.psum(local_gram, "fsdp")
    lower_factor = jnp.linalg.cholesky(gram_matrix)
    solved = jax.scipy.linalg.solve_triangular(lower_factor, left_factor.T, lower=True)
    orthonormal = solved.T.astype(jnp.bfloat16)
    right_share = lax.psum_scatter(
        lax.dot_general(
            orthonormal, blended, (((0,), (0,)), ((), ())), preferred_element_type=jnp.float32
        ).astype(jnp.bfloat16),
        "fsdp",
        scatter_dimension=0,
        tiled=True,
    ).astype(jnp.float32)
    square_sums = lax.psum(jnp.sum(right_share * right_share, axis=1), "tensor")
    own_inverse = lax.rsqrt(square_sums + epsilon)
    own_factor = (right_share * own_inverse[:, None]).T
    right_rows, inverse = (
        lax.all_gather(right_share, "fsdp", axis=0, tiled=True),
        lax.all_gather(own_inverse, "fsdp", axis=0, tiled=True),
    )
    full_rows = right_rows * inverse[:, None]
    product = jnp.dot(
        orthonormal, right_rows.astype(jnp.bfloat16), preferred_element_type=jnp.float32
    )
    stepped = jnp.dot(
        orthonormal, full_rows.astype(jnp.bfloat16), preferred_element_type=jnp.float32
    )
    new_momentum = (blended.astype(jnp.float32) - (1.0 - decay_rate) * product).astype(jnp.bfloat16)
    update = (stepped * jnp.sqrt(jnp.float32(D * FF / R))).astype(jnp.bfloat16)
    return (new_momentum, own_factor, update)


def solution(mesh):
    placed = (P("fsdp", "tensor"), P("fsdp", "tensor"), P("tensor", "fsdp"))
    return jax.shard_map(
        on_device,
        mesh=mesh,
        in_specs=placed,
        out_specs=(P("fsdp", "tensor"), P("tensor", "fsdp"), P("fsdp", "tensor")),
        check_vma=False,
    )
```

profile of v0, /device:TPU:0, one launch (start us, length us, event | category | flops | bytes accessed | tf_op | source)
XLA Modules:
  0.0 598.9 jit_solution(7872715118207155491)
XLA Ops:
  7.2 0.0 all-gather.4.cloned.1.call-start
  7.2 2.5 convert_element_type.39
  9.7 0.0 all-reduce.4.cloned.1.call-start
  9.8 33.1 %all-gather.4.cloned.1.call-done = bf16[1792,512]{1,0:T(8,128)(2,1)} async-done(((bf16[1792,256]{1,0:T(8,128)(2,1)}), bf16[1792,512]{1,0:T(8,128)(2,1)}) %all-gather.4.cloned.1.call-update) | async-done | bytes 1835024 | tf_op jit(solution)/shard_map/all_gather | solution.py:20
  42.9 15.9 %fusion.35 = f32[4096,512]{1,0:T(8,128)} fusion(bf16[1792,512]{1,0:T(8,128)(2,1)} %all-gather.4.cloned.1.call-done, bf16[4096,1792]{1,0:T(8,128)(2,1)} %param.4, bf16[4096,1792]{1,0:T(8,128)(2,1)} %param.3), kind=kOutput, calls=%fused_computation.77 | convolution fusion | flops 7545552896 | bytes 39583744 | tf_op jit(solution)/shard_map/dot_general | solution.py:18
  58.8 0.0 all-reduce.6.cloned.1.call-start
  58.9 170.2 %all-reduce.4.cloned.1.call-done = f32[4096,512]{1,0:T(8,128)} async-done(((f32[4096,512]{1,0:T(8,128)}), f32[4096,512]{1,0:T(8,128)}) %all-reduce.4.cloned.1.call-update) | async-done | bytes 8388624 | tf_op jit(solution)/shard_map/psum | solution.py:23
  229.1 18.5 %fusion.40 = f32[512,512]{0,1:T(8,128)} fusion(f32[4096,512]{1,0:T(8,128)} %all-reduce.4.cloned.1.call-done), kind=kOutput, calls=%fused_computation.82 | convolution fusion | flops 12884901888 | bytes 9437184 | tf_op jit(solution)/shard_map/dot_general | solution.py:24
  247.6 0.5 reduce-scatter.2.cloned.1.call-start
  248.1 39.6 %all-reduce.6.cloned.1.call-done = f32[512,512]{0,1:T(8,128)} async-done(((f32[512,512]{0,1:T(8,128)}), f32[512,512]{0,1:T(8,128)}) %all-reduce.6.cloned.1.call-update) | async-done | bytes 1048592 | tf_op jit(solution)/shard_map/psum | solution.py:27
  287.7 1.6 copy.10
  289.2 1.4 fusion.16
  290.7 11.7 %cholesky.104 = f32[128,128]{1,0:T(8,128)S(1)} custom-call(f32[128,128]{1,0:T(8,128)S(1)} %cholesky.266), custom_call_target="Cholesky" | custom-call | tf_op jit(solution)/shard_map/jit(cholesky)/cholesky | solution.py:28
  302.4 9.8 %custom-call.31 = f32[1,128,128]{1,2,0:T(8,128)S(1)} custom-call(f32[1,128,128]{2,1,0:T(8,128)S(1)} %get-tuple-element.36), custom_call_target="InvertDiagBlocksLowerTriangular" | custom-call | tf_op jit(solution)/shard_map/jit(cholesky)/cholesky | solution.py:28
  312.3 0.1 cholesky.224
  312.4 0.3 constant_dynamic-update-slice_fusion.3
  312.7 0.3 convolution_subtract_fusion.2
  313.1 11.7 %cholesky.217 = f32[128,128]{1,0:T(8,128)S(1)} custom-call(f32[128,128]{1,0:T(8,128)S(1)} %cholesky.270), custom_call_target="Cholesky" | custom-call | tf_op jit(solution)/shard_map/jit(cholesky)/cholesky | solution.py:28
  324.8 10.0 %custom-call.32 = f32[1,128,128]{1,2,0:T(8,128)S(1)} custom-call(f32[1,128,128]{2,1,0:T(8,128)S(1)} %get-tuple-element.33), custom_call_target="InvertDiagBlocksLowerTriangular" | custom-call | tf_op jit(solution)/shard_map/jit(cholesky)/cholesky | solution.py:28
  334.8 0.3 convolution_dynamic-update-slice_fusion
  335.0 0.4 convolution_subtract_fusion.3
  335.4 11.7 %cholesky.238 = f32[128,128]{1,0:T(8,128)S(1)} custom-call(f32[128,128]{1,0:T(8,128)S(1)} %cholesky.275), custom_call_target="Cholesky" | custom-call | tf_op jit(solution)/shard_map/jit(cholesky)/cholesky | solution.py:28
  347.2 0.6 compare_reduce_fusion.1
  347.8 9.8 %custom-call.33 = f32[1,128,128]{1,2,0:T(8,128)S(1)} custom-call(f32[1,128,128]{2,1,0:T(8,128)S(1)} %get-tuple-element.30), custom_call_target="InvertDiagBlocksLowerTriangular" | custom-call | tf_op jit(solution)/shard_map/jit(cholesky)/cholesky | solution.py:28
  357.6 0.2 convolution_dynamic-update-slice_fusion.1
  357.8 0.4 convolution_subtract_fusion.4
  358.2 11.7 %cholesky.255 = f32[128,128]{1,0:T(8,128)S(1)} custom-call(f32[128,128]{1,0:T(8,128)S(1)} %convolution_subtract_fusion.4), custom_call_target="Cholesky" | custom-call | tf_op jit(solution)/shard_map/jit(cholesky)/cholesky | solution.py:28
  370.0 0.7 compare_reduce_fusion
  370.6 0.6 compare_reduce_fusion.2
  373.8 0.5 select_select_fusion
  374.3 8.0 %while.1 = (s32[]{:T(128)}, f32[512,512]{1,0:T(8,128)S(1)}, s32[4,2]{0,1:T(2,128)S(1)}, f32[4,128,128]{2,1,0:T(8,128)S(1)}, s32[]{:T(128)}) while((s32[]{:T(128)}, f32[512,512]{1,0:T(8,128)S(1)}, s32[4,2]{0,1:T(2,128)S(1)}, f32[4,128,128]{2,1,0:T(8,128)S(1)}, s32[]{:T(128)}) %tuple.36), condition=%wide.while_cond, body=%wide.while_body.sunk | while | flops 2 | bytes 131189 | solution.py:29
  374.3 0.1 constant_dynamic-slice_fusion.2
  374.4 0.5 fusion.50
  374.9 1.4 bitcast_dynamic-update-slice_fusion.2
  376.3 0.1 constant_dynamic-slice_fusion.2
  376.4 0.5 fusion.50
  376.9 1.4 bitcast_dynamic-update-slice_fusion.2
  378.3 0.1 constant_dynamic-slice_fusion.2
  378.4 0.5 fusion.50
  378.9 1.4 bitcast_dynamic-update-slice_fusion.2
  380.3 0.1 constant_dynamic-slice_fusion.2
  380.4 0.5 fusion.50
  380.9 1.4 bitcast_dynamic-update-slice_fusion.2
  382.3 39.3 %custom-call.34 = f32[4,128,128]{1,2,0:T(8,128)S(1)} custom-call(f32[4,128,128]{2,1,0:T(8,128)S(1)} %get-tuple-element.10), custom_call_target="InvertDiagBlocksLowerTriangular" | custom-call | tf_op jit(solution)/shard_map/jit(_solve_triangular)/triangular_solve | solution.py:29
  421.7 3.7 fusion.39
  425.4 5.5 convolution_subtract_fusion.1
  430.9 3.0 fusion.38
  433.9 7.3 %convolution_subtract_fusion = f32[128,4096]{0,1:T(8,128)S(1)} fusion(f32[128,4096]{1,0:T(8,128)S(1)} %get-tuple-element.42, f32[128,4096]{1,0:T(8,128)S(1)} %get-tuple-element.44, f32[512,4096]{0,1:T(8,128)S(1)} %bitcast.66, f32[512,512]{1,0:T(8,128)S(1)} %get-tuple-element.107), kind=kOutput, calls=%fused_computation.11 | convolution fusion | flops 1612185600 | bytes 8519680 | tf_op jit(solution)/shard_map/jit(_solve_triangular)/triangular_solve | solution.py:29
  441.3 2.9 fusion.37
  444.2 10.8 %fusion.6 = f32[128,4096]{0,1:T(8,128)S(1)} fusion(f32[128,4096]{1,0:T(8,128)S(1)} %get-tuple-element.40, f32[128,4096]{1,0:T(8,128)S(1)} %get-tuple-element.42, f32[128,4096]{1,0:T(8,128)S(1)} %get-tuple-element.44, f32[512,4096]{0,1:T(8,128)S(1)} %bitcast.67, f32[512,512]{1,0:T(8,128)S(1)} %get-tuple-element.107), kind=kOutput, calls=%fused_computation.13 | convolution fusion | flops 2419589120 | bytes 10682368 | tf_op jit(solution)/shard_map/jit(_solve_triangular)/triangular_solve | solution.py:29
  455.0 1.9 convolution_convert_fusion
  456.9 16.1 %convolution_convert_fusion.1 = bf16[512,1792]{1,0:T(8,128)(2,1)} fusion(bf16[128,4096]{1,0:T(8,128)(2,1)S(1)} %convolution_convert_fusion, bf16[128,4096]{1,0:T(8,128)(2,1)} %get-tuple-element.39, bf16[128,4096]{1,0:T(8,128)(2,1)} %get-tuple-element.41, bf16[128,4096]{1,0:T(8,128)(2,1)S(1)} %get-tuple-element.43, bf16[4096,1792]{1,0:T(8,128)(2,1)} %param.4, ...), kind=kOutput, calls=%fused_computation.20 | convolution fusion | flops 7563247616 | bytes 35389440 | tf_op jit(solution)/shard_map/dot_general | solution.py:32
  473.0 0.0 reduce-scatter.2.cloned.1.call-update
  473.0 0.0 all-gather.6.cloned.1.call-start
  473.1 29.1 %reduce-scatter.2.cloned.1.call-done = bf16[256,1792]{1,0:T(8,128)(2,1)} async-done(((bf16[512,1792]{1,0:T(8,128)(2,1)}), bf16[256,1792]{1,0:T(8,128)(2,1)}) %reduce-scatter.2.cloned.1.call-update) | async-done | bytes 917520 | tf_op jit(solution)/shard_map/reduce_scatter | solution.py:31
  502.2 2.6 convert_element_type.41
  504.9 0.3 multiply_reduce_fusion
  505.1 33.0 %psum.23 = f32[256]{0:T(256)S(1)} all-reduce(f32[256]{0:T(256)S(1)} %multiply_reduce_fusion), channel_id=1, replica_groups=mesh['fsdp'=2,'tensor'=16] {'tensor'}, use_global_device_ids=true, to_apply=%region_12.13 | all-reduce | flops 256 | bytes 2048 | tf_op jit(solution)/shard_map/psum | solution.py:39
  538.1 0.2 multiply_bitcast_fusion
  538.3 1.7 copy.11
  540.0 4.4 all-gather
  544.4 11.5 %all-gather.6.cloned.1.call-done = f32[512,1792]{1,0:T(8,128)} async-done(((f32[256,1792]{1,0:T(8,128)}), f32[512,1792]{1,0:T(8,128)}) %all-gather.6.cloned.1.call-update) | async-done | bytes 3670032 | tf_op jit(solution)/shard_map/all_gather | solution.py:43
  555.9 22.5 %subtract_convert_fusion = bf16[4096,1792]{1,0:T(8,128)(2,1)} fusion(f32[512,1792]{1,0:T(8,128)} %all-gather.6.cloned.1.call-done, bf16[128,4096]{1,0:T(8,128)(2,1)} %copy-done.1, bf16[128,4096]{1,0:T(8,128)(2,1)} %get-tuple-element.39, bf16[128,4096]{1,0:T(8,128)(2,1)} %get-tuple-element.41, bf16[128,4096]{1,0:T(8,128)(2,1)} %copy-done.3, ...), kind=kOutput, calls=%fused_computation.3 | convolution fusion | flops 7592607744 | bytes 51904512 | tf_op jit(solution)/shard_map/dot_general | solution.py:47
  578.4 13.5 %multiply_convert_fusion = bf16[4096,1792]{1,0:T(8,128)(2,1)} fusion(f32[512,1792]{1,0:T(8,128)} %all-gather.6.cloned.1.call-done, f32[512]{0:T(512)S(1)} %bitcast.69, bf16[128,4096]{1,0:T(8,128)(2,1)S(1)} %copy-done.2, bf16[128,4096]{1,0:T(8,128)(2,1)} %get-tuple-element.39, bf16[128,4096]{1,0:T(8,128)(2,1)S(1)} %copy-done.5, ...), kind=kOutput, calls=%fused_computation.2 | convolution fusion | flops 7549485056 | bytes 22546432 | tf_op jit(solution)/shard_map/dot_general | solution.py:50
  (32 shorter events, 0.3 us)
Async XLA Ops:
  7.2 35.8 %all-gather.4.cloned.1.call-start = ((), (), s32[]{:S(2)}) async-start(), calls=%async_computation.1 | async-start | bytes 2752512 | tf_op jit(solution)/shard_map/all_gather | solution.py:20
  9.7 219.3 %all-reduce.4.cloned.1.call-start = ((), (), s32[]{:S(2)}) async-start(), calls=%async_computation.2 | async-start | bytes 16777216 | tf_op jit(solution)/shard_map/psum | solution.py:23
  58.8 228.8 %all-reduce.6.cloned.1.call-start = ((), (), s32[]{:S(2)}) async-start(), calls=%async_computation.3 | async-start | bytes 2097152 | tf_op jit(solution)/shard_map/psum | solution.py:27
  247.6 254.7 %reduce-scatter.2.cloned.1.call-start = ((), (), s32[]{:S(2)}) async-start(), calls=%async_computation.4 | async-start | bytes 2752512 | tf_op jit(solution)/shard_map/reduce_scatter | solution.py:31
  421.6 12.3 %slice-start = ((s8[8388608]{0:T(1024)(128)(4,1)}), s8[4194304]{0:T(1024)(128)(4,1)S(1)}, s32[]{:S(2)}) async-start(s8[8388608]{0:T(1024)(128)(4,1)} %bitcast.64), calls=%async_computation.6 | async-start | bytes 8388608
  425.3 31.6 %copy-start.3 = (bf16[128,4096]{1,0:T(8,128)(2,1)}, bf16[128,4096]{1,0:T(8,128)(2,1)S(1)}, u32[]{:S(2)}) copy-start(bf16[128,4096]{1,0:T(8,128)(2,1)S(1)} %get-tuple-element.43) | copy-start | bytes 3145732
  425.4 8.6 %slice-start.1 = ((s8[8388608]{0:T(1024)(128)(4,1)}), s8[4194304]{0:T(1024)(128)(4,1)S(1)}, s32[]{:S(2)}) async-start(s8[8388608]{0:T(1024)(128)(4,1)} %bitcast.64), calls=%async_computation.7 | async-start | bytes 8388608
  456.9 16.1 %copy-start.1 = (bf16[128,4096]{1,0:T(8,128)(2,1)}, bf16[128,4096]{1,0:T(8,128)(2,1)S(1)}, u32[]{:S(2)}) copy-start(bf16[128,4096]{1,0:T(8,128)(2,1)S(1)} %convolution_convert_fusion) | copy-start | bytes 3145732
  473.0 82.8 %all-gather.6.cloned.1.call-start = ((), (), s32[]{:S(2)}) async-start(), calls=%async_computation.5 | async-start | bytes 5505024 | tf_op jit(solution)/shard_map/all_gather | solution.py:43
  502.2 2.6 copy-start
  544.4 34.0 %copy-start.2 = (bf16[128,4096]{1,0:T(8,128)(2,1)S(1)}, bf16[128,4096]{1,0:T(8,128)(2,1)}, u32[]{:S(2)}) copy-start(bf16[128,4096]{1,0:T(8,128)(2,1)} %copy-done.1) | copy-start | bytes 3145732
  544.4 34.0 %copy-start.4 = (bf16[128,4096]{1,0:T(8,128)(2,1)S(1)}, bf16[128,4096]{1,0:T(8,128)(2,1)}, u32[]{:S(2)}) copy-start(bf16[128,4096]{1,0:T(8,128)(2,1)} %copy-done.3) | copy-start | bytes 3145732
  544.4 34.0 %copy-start.5 = (bf16[128,4096]{1,0:T(8,128)(2,1)S(1)}, bf16[128,4096]{1,0:T(8,128)(2,1)}, u32[]{:S(2)}) copy-start(bf16[128,4096]{1,0:T(8,128)(2,1)} %get-tuple-element.41) | copy-start | bytes 3145732
Sparse Core Ops, SparseCore 0:
  10.1 32.8 all-gather.3
  59.0 170.0 all-reduce.3
  247.7 39.9 all-reduce.5
  473.2 29.0 reduce-scatter.1
  505.0 50.8 all-gather.5
where the time goes:
time: 605 us; the launch traced here: 599 us
  waiting for transfers between devices  284 us (47%)
  other arithmetic  125 us (21%)
  matrix products  124 us (20%)
  blocking collectives  37.4 us (6%)
  between operations  17 us (3%)
  local copies, waits for them, and re-layouts  11.3 us (2%)
    psum x1, waiting for transfers between devices, on_device(): left_factor = lax.psum(partial_left, 'tensor')  170 us
    another operation x14, other arithmetic, on_device(): lower_factor = jnp.linalg.cholesky(gram_matrix)  78.5 us
    another operation x3, other arithmetic, on_device(): jax.scipy.linalg.solve_triangular(lower_factor, left_factor.T, lower=True)  39.9 us
    psum x1, waiting for transfers between devices, on_device(): gram_matrix = lax.psum(local_gram, 'fsdp')  39.6 us
    another operation x7, matrix products, on_device(): jax.scipy.linalg.solve_triangular(lower_factor, left_factor.T, lower=True)  35.2 us
    all_gather x1, waiting for transfers between devices, on_device(): lax.all_gather(lowered, 'fsdp', axis=1, tiled=True)  33.1 us
    psum x1, blocking collectives, on_device(): square_sums = lax.psum(jnp.sum(right_share * right_share, axis=1), 'tensor')  33 us
    reduce_scatter x1, waiting for transfers between devices, on_device(): lax.psum_scatter(lax.dot_general(orthonormal, blended, (((0,), (0,)), (()...  29.1 us
  transfers between devices with their start and end apart: 5, of which 5 were waited for; matrix products, arithmetic and copies ran while one was open for 0% of the time, Pallas kernels for 0%

commit v1 on v0

v1 whole, which is shorter than its diff:
```python
import jax
import jax.numpy as jnp
from jax import lax
from jax.experimental import pallas as pl
from jax.experimental.pallas import tpu as pltpu
from jax.sharding import PartitionSpec as P

decay_rate = 0.95
epsilon = 1e-06
BLOCK = 128


def inverse_kernel(gram_ref, out_ref, state):
    rank = gram_ref.shape[0]
    rows = lax.broadcasted_iota(jnp.int32, (rank, rank), 0)
    columns = lax.broadcasted_iota(jnp.int32, (rank, rank), 1)
    state[:, :rank] = gram_ref[...]
    state[:, rank:] = (rows == columns).astype(jnp.float32)
    r_in = lax.broadcasted_iota(jnp.int32, (BLOCK, BLOCK), 0)
    c_in = lax.broadcasted_iota(jnp.int32, (BLOCK, BLOCK), 1)
    wide = lax.broadcasted_iota(jnp.int32, (BLOCK, rank), 1)

    @pl.loop(0, rank // BLOCK)
    def _(b):
        at = pl.multiple_of(b * BLOCK, BLOCK)
        a = state[pl.ds(at, BLOCK), pl.ds(at, BLOCK)]
        v = (r_in == c_in).astype(jnp.float32)
        for j in range(BLOCK - 1):
            lo = (j + 1) // 8 * 8
            top = a[lo:, :]
            scale = 1.0 / a[j : j + 1, j : j + 1]
            factor = jnp.where(r_in[lo:, :1] > j, top[:, j : j + 1] * scale, 0.0)
            new_a = top - factor * a[j : j + 1, :]
            new_v = v[lo:, :] - factor * v[j : j + 1, :]
            a = new_a if lo == 0 else jnp.concatenate([a[:lo], new_a], axis=0)
            v = new_v if lo == 0 else jnp.concatenate([v[:lo], new_v], axis=0)
        diagonal = jnp.sum(jnp.where(r_in == c_in, a, 0.0), axis=1, keepdims=True)
        block_inverse = v * (1.0 / jnp.sqrt(diagonal))
        solved = jnp.dot(
            block_inverse,
            state[pl.ds(at, BLOCK), :],
            precision=lax.Precision.HIGHEST,
            preferred_element_type=jnp.float32,
        )
        out_ref[pl.ds(at, BLOCK), :] = solved[:, rank:]
        lower = jnp.where(wide >= at + BLOCK, solved[:, :rank], 0.0)
        state[...] = state[...] - lax.dot_general(
            lower,
            solved,
            (((0,), (0,)), ((), ())),
            precision=lax.Precision.HIGHEST,
            preferred_element_type=jnp.float32,
        )


def inverse_of_lower(gram):
    rank = gram.shape[0]
    return pl.pallas_call(
        inverse_kernel,
        out_shape=jax.ShapeDtypeStruct((rank, rank), jnp.float32),
        in_specs=[pl.BlockSpec(memory_space=pltpu.VMEM)],
        out_specs=pl.BlockSpec(memory_space=pltpu.VMEM),
        scratch_shapes=[pltpu.VMEM((rank, 2 * rank), jnp.float32)],
        compiler_params=pltpu.CompilerParams(vmem_limit_bytes=32 << 20),
        cost_estimate=pl.CostEstimate(flops=40_000_000_000, bytes_accessed=2 << 20, transcendentals=0),
    )(gram)


def butterfly(value, axis, size):
    if size & (size - 1):
        return lax.psum(value, axis)
    step = 1
    while step < size:
        value = value + lax.ppermute(value, axis, [(i, i ^ step) for i in range(size)])
        step *= 2
    return value


def on_device(halves, spread, momentum, gradient, factor):
    whole_rows = momentum.shape[0] * halves
    whole_columns = momentum.shape[1] * spread
    own_rank = factor.shape[1]
    rank = own_rank * halves
    place = lax.axis_index("fsdp")
    swap = [(0, 1), (1, 0)]

    blended = (momentum.astype(jnp.float32) + gradient.astype(jnp.float32)).astype(jnp.bfloat16)
    lowered = factor.astype(jnp.bfloat16)

    def summed_rows(columns):
        part = jnp.dot(blended, columns, preferred_element_type=jnp.float32).astype(jnp.bfloat16)
        return lax.psum_scatter(part, "tensor", scatter_dimension=0, tiled=True)

    if halves == 2:
        other = lax.ppermute(lowered, "fsdp", swap)
        mine = summed_rows(lowered)
        theirs = summed_rows(other)
        rows = jnp.where(
            place == 0,
            jnp.concatenate([mine, theirs], axis=1),
            jnp.concatenate([theirs, mine], axis=1),
        )
    else:
        rows = summed_rows(lax.all_gather(lowered, "fsdp", axis=1, tiled=True))

    gram = lax.psum(
        lax.dot_general(rows, rows, (((0,), (0,)), ((), ())), preferred_element_type=jnp.float32),
        ("fsdp", "tensor"),
    )
    left = lax.all_gather(rows, "tensor", axis=0, tiled=True)
    lower_inverse = inverse_of_lower(gram)
    high = lower_inverse.astype(jnp.bfloat16)
    low = (lower_inverse - high.astype(jnp.float32)).astype(jnp.bfloat16)
    across = (((1,), (1,)), ((), ()))
    orthonormal = (
        lax.dot_general(left, high, across, preferred_element_type=jnp.float32)
        + lax.dot_general(left, low, across, preferred_element_type=jnp.float32)
    ).astype(jnp.bfloat16)

    share = lax.dot_general(
        orthonormal, blended, (((0,), (0,)), ((), ())), preferred_element_type=jnp.float32
    ).astype(jnp.bfloat16)
    if halves == 2:
        right = share.astype(jnp.float32) + lax.ppermute(share, "fsdp", swap).astype(jnp.float32)
    else:
        right = lax.psum(share, "fsdp").astype(jnp.float32)
    square_sums = butterfly(jnp.sum(right * right, axis=1), "tensor", spread)
    inverse = lax.rsqrt(square_sums + epsilon)
    normal = right * inverse[:, None]
    own_factor = lax.dynamic_slice_in_dim(normal, place * own_rank, own_rank, axis=0).T
    product = jnp.dot(orthonormal, right.astype(jnp.bfloat16), preferred_element_type=jnp.float32)
    new_momentum = (blended.astype(jnp.float32) - (1.0 - decay_rate) * product).astype(jnp.bfloat16)
    stepped = jnp.dot(orthonormal, normal.astype(jnp.bfloat16), preferred_element_type=jnp.float32)
    scale = jnp.sqrt(jnp.float32(whole_rows * whole_columns / rank))
    update = (stepped * scale).astype(jnp.bfloat16)
    return (new_momentum, own_factor, update)


def solution(mesh):
    halves, spread = mesh.shape["fsdp"], mesh.shape["tensor"]

    def body(momentum, gradient, factor):
        return on_device(halves, spread, momentum, gradient, factor)

    return jax.shard_map(
        body,
        mesh=mesh,
        in_specs=(P("fsdp", "tensor"), P("fsdp", "tensor"), P("tensor", "fsdp")),
        out_specs=(P("fsdp", "tensor"), P("tensor", "fsdp"), P("fsdp", "tensor")),
        check_vma=False,
    )
```

time: 605 us -> 462 us (0.76)
  other arithmetic: 125 us -> 17.2 us
  matrix products: 124 us -> 64.4 us
  Pallas kernels: 0 us -> 51.8 us
  blocking collectives: 37.4 us -> 0 us
  waiting for transfers between devices: 284 us -> 295 us
  starting transfers between devices: 0.67 us -> 9.21 us
    another operation x17 -> x0, other arithmetic: 118 us -> none  [the longest x14 78.5 us: on_device(): lower_factor = jnp.linalg.cholesky(gram_matrix)]
    psum x2 -> x1, waiting for transfers between devices: 210 us -> 132 us  [on_device(): lax.psum(lax.dot_general(rows, rows, (((0,), (0,)), ((), ())), preferred_...]
    reduce_scatter x1 -> x2, waiting for transfers between devices: 29.1 us -> 95.8 us  [summed_rows(): return lax.psum_scatter(part, 'tensor', scatter_dimension=0, tiled=True)]
    ppermute x0 -> x6, waiting for transfers between devices: none -> 66.2 us  [the longest x1 40 us: on_device(): lax.ppermute(share, 'fsdp', swap).astype(jnp.float32)]
    pallas_call x0 -> x1, Pallas kernels: none -> 51.8 us  [inverse_of_lower(): pl.pallas_call(inverse_kernel, out_shape=jax.ShapeDtypeStruct((rank, rank...]
    all_gather x2 -> x1, waiting for transfers between devices: 44.6 us -> 0.02 us  [on_device(): left = lax.all_gather(rows, 'tensor', axis=0, tiled=True)]
    another operation x13 -> x0, matrix products: 37.1 us -> none  [the longest x7 35.2 us: on_device(): jax.scipy.linalg.solve_triangular(lower_factor, left_factor.T, lower=True)]
    psum x1 -> x0, blocking collectives: 33 us -> none  [on_device(): square_sums = lax.psum(jnp.sum(right_share * right_share, axis=1), 'tensor')]
  transfers between devices with their start and end apart: 5 -> 10, of which waited for: 5 -> 8; matrix products, arithmetic and copies ran while one was open for 0% -> 6% of each run, Pallas kernels for 0% -> 11%
where the time goes in v1:
time: 462 us; the launch traced here: 461 us
  waiting for transfers between devices  295 us (64%)
  matrix products  64.4 us (14%)
  Pallas kernels  51.8 us (11%)
  other arithmetic  17.2 us (4%)
  between operations  13.9 us (3%)
  local copies, waits for them, and re-layouts  10.3 us (2%)
  starting transfers between devices  9.21 us (2%)
    psum x1, waiting for transfers between devices, on_device(): lax.psum(lax.dot_general(rows, rows, (((0,), (0,)), ((), ())), preferred_...  132 us
    reduce_scatter x2, waiting for transfers between devices, summed_rows(): return lax.psum_scatter(part, 'tensor', scatter_dimension=0, tiled=True)  95.8 us
    pallas_call x1, Pallas kernels, inverse_of_lower(): pl.pallas_call(inverse_kernel, out_shape=jax.ShapeDtypeStruct((rank, rank...  51.8 us
    ppermute x1, waiting for transfers between devices, on_device(): lax.ppermute(share, 'fsdp', swap).astype(jnp.float32)  40 us
    ppermute x1, waiting for transfers between devices, on_device(): other = lax.ppermute(lowered, 'fsdp', swap)  20.4 us
    dot_general x2, matrix products, summed_rows(): jnp.dot(blended, columns, preferred_element_type=jnp.float32)  15.8 us
    dot_general x1, matrix products, on_device(): jnp.dot(orthonormal, right.astype(jnp.bfloat16), preferred_element_type=j...  15.7 us
    dot_general x1, matrix products, on_device(): lax.dot_general(orthonormal, blended, (((0,), (0,)), ((), ())), preferred...  13.8 us
  transfers between devices with their start and end apart: 10, of which 8 were waited for; matrix products, arithmetic and copies ran while one was open for 6% of the time, Pallas kernels for 11%

profile of v1, /device:TPU:0, one launch (start us, length us, event | category | flops | bytes accessed | tf_op | source)
XLA Modules:
  0.0 461.5 jit_solution(949954754372182483)
XLA Ops:
  7.2 0.0 reduce-scatter.3.cloned.1.call-start
  7.2 1.6 convert_element_type.58
  8.8 11.6 %add_convert_fusion = bf16[4096,1792]{1,0:T(8,128)(2,1)S(1)} fusion(bf16[4096,1792]{1,0:T(8,128)(2,1)} %param.4, bf16[4096,1792]{1,0:T(8,128)(2,1)} %param.3), kind=kLoop, calls=%fused_computation.2 | loop fusion | flops 29360128 | bytes 44040192 | tf_op jit(solution)/shard_map/convert_element_type | solution.py:87
  20.4 0.0 copy-start.2
  20.4 5.5 %copy-done.2 = bf16[4096,1792]{1,0:T(8,128)(2,1)} copy-done((bf16[4096,1792]{1,0:T(8,128)(2,1)}, bf16[4096,1792]{1,0:T(8,128)(2,1)S(1)}, u32[]{:S(2)}) %copy-start.2) | copy-done | bytes 14680088
  25.9 5.3 %convolution_convert_fusion.1 = bf16[4096,256]{1,0:T(8,128)(2,1)} fusion(bf16[4096,1792]{1,0:T(8,128)(2,1)S(1)} %add_convert_fusion, bf16[1792,256]{1,0:T(8,128)(2,1)S(1)} %convert_element_type.58), kind=kOutput, calls=%fused_computation.5 | convolution fusion | flops 3759144960 | bytes 17694720 | tf_op jit(solution)/shard_map/dot_general | solution.py:91
  31.2 0.0 reduce-scatter.3.cloned.1.call-update
  31.2 0.0 reduce-scatter.5.cloned.1.call-start
  31.3 3.1 collective-permute-start
  34.3 20.4 %collective-permute-done = bf16[1792,256]{1,0:T(8,128)(2,1)S(1)} collective-permute-done((bf16[1792,256]{1,0:T(8,128)(2,1)S(1)}, bf16[1792,256]{1,0:T(8,128)(2,1)S(1)}, u32[]{:S(2)}, u32[]{:S(2)}) %collective-permute-start) | collective-permute-done | bytes 917536 | tf_op jit(solution)/shard_map/ppermute | solution.py:95
  54.7 10.5 %convolution_convert_fusion = bf16[4096,256]{1,0:T(8,128)(2,1)} fusion(bf16[4096,1792]{1,0:T(8,128)(2,1)} %copy-done.2, bf16[1792,256]{1,0:T(8,128)(2,1)S(1)} %collective-permute-done), kind=kOutput, calls=%fused_computation.4 | convolution fusion | flops 3759144960 | bytes 17694720 | tf_op jit(solution)/shard_map/dot_general | solution.py:91
  65.2 0.0 reduce-scatter.5.cloned.1.call-update
  65.2 0.0 all-reduce.2.cloned.1.call-start
  65.3 30.7 %reduce-scatter.3.cloned.1.call-done = bf16[256,256]{1,0:T(8,128)(2,1)} async-done(((bf16[4096,256]{1,0:T(8,128)(2,1)}), bf16[256,256]{1,0:T(8,128)(2,1)}) %reduce-scatter.3.cloned.1.call-update) | async-done | bytes 131088 | tf_op jit(solution)/shard_map/reduce_scatter | solution.py:92
  95.9 65.1 %reduce-scatter.5.cloned.1.call-done = bf16[256,256]{1,0:T(8,128)(2,1)} async-done(((bf16[4096,256]{1,0:T(8,128)(2,1)}), bf16[256,256]{1,0:T(8,128)(2,1)}) %reduce-scatter.5.cloned.1.call-update) | async-done | bytes 131088 | tf_op jit(solution)/shard_map/reduce_scatter | solution.py:92
  161.0 1.2 maximum_select_fusion
  162.2 0.0 copy-start.6
  162.2 1.3 fusion.7
  163.5 0.0 all-reduce.2.cloned.1.call-update
  163.5 0.2 all-gather.2.cloned.1.call-start
  163.7 0.0 copy-done.6
  163.8 0.3 all-gather.2.cloned.1.call-update
  164.1 132.3 %all-reduce.2.cloned.1.call-done.gram_ref = f32[512,512]{1,0:T(8,128)} async-done(((f32[512,512]{1,0:T(8,128)}), f32[512,512]{1,0:T(8,128)}) %all-reduce.2.cloned.1.call-update) | async-done | bytes 1048592 | tf_op jit(solution)/shard_map/psum | solution.py:106
  296.4 0.0 copy-start
  296.4 1.2 copy-done
  297.6 51.8 %shard_map.58 = f32[512,512]{1,0:T(8,128)S(1)} custom-call(f32[512,512]{1,0:T(8,128)S(1)} %copy-done), custom_call_target="tpu_custom_call" | custom-call | flops 40000000000 | bytes 2097152 | tf_op jit(solution)/shard_map/pallas_call | solution.py:58
  349.4 0.0 all-gather.2.cloned.1.call-done
  349.4 0.0 copy-start.1
  349.4 4.9 %fusion.5 = f32[4096,512]{1,0:T(8,128)S(1)} fusion(bf16[4096,512]{1,0:T(8,128)(2,1)} %all-gather.2.cloned.1.call-done, f32[512,512]{1,0:T(8,128)S(1)} %shard_map.58), kind=kOutput, calls=%fused_computation.16 | convolution fusion | flops 2147745792 | bytes 13631488 | tf_op jit(solution)/shard_map/dot_general | solution.py:116
  354.4 0.0 copy-done.1
  354.4 2.5 add_convert_fusion.1
  356.8 0.0 copy-start.3
  356.9 13.8 %convolution_convert_fusion.2 = bf16[512,1792]{1,0:T(8,128)(2,1)S(1)} fusion(bf16[4096,512]{1,0:T(8,128)(2,1)S(1)} %add_convert_fusion.1, bf16[4096,1792]{1,0:T(8,128)(2,1)} %copy-done.2), kind=kOutput, calls=%fused_computation.10 | convolution fusion | flops 7517110272 | bytes 20709376 | tf_op jit(solution)/shard_map/dot_general | solution.py:120
  370.6 0.0 copy-done.3
  370.6 1.5 collective-permute-start.1
  372.2 40.0 %collective-permute-done.1 = bf16[512,1792]{1,0:T(8,128)(2,1)S(1)} collective-permute-done((bf16[512,1792]{1,0:T(8,128)(2,1)S(1)}, bf16[512,1792]{1,0:T(8,128)(2,1)S(1)}, u32[]{:S(2)}, u32[]{:S(2)}) %collective-permute-start.1) | collective-permute-done | bytes 1835040 | tf_op jit(solution)/shard_map/ppermute | solution.py:124
  412.1 0.0 copy-start.5
  412.1 1.2 copy-done.5
  413.3 0.7 multiply_reduce_fusion
  414.0 0.1 collective-permute-start.2
  414.1 1.1 collective-permute-done.2
  415.2 1.0 collective-permute-start.3
  416.2 2.6 collective-permute-done.3
  418.8 1.5 collective-permute-start.4
  420.3 2.1 collective-permute-done.4
  422.4 1.8 collective-permute-start.5
  424.2 15.7 %subtract_convert_fusion = bf16[4096,1792]{1,0:T(8,128)(2,1)} fusion(bf16[4096,1792]{1,0:T(8,128)(2,1)} %copy-done.2, bf16[4096,512]{1,0:T(8,128)(2,1)} %copy-done.3, bf16[512,1792]{1,0:T(8,128)(2,1)} %copy-done.5, bf16[512,1792]{1,0:T(8,128)(2,1)S(1)} %convolution_convert_fusion.2), kind=kOutput, calls=%fused_computation.1 | convolution fusion | flops 7549222912 | bytes 37224448 | tf_op jit(solution)/shard_map/dot_general | solution.py:131
  439.9 0.0 copy-start.4
  439.9 0.0 collective-permute-done.5
  439.9 2.2 fusion
  442.1 0.6 copy-done.4
  442.6 10.5 %multiply_convert_fusion = bf16[4096,1792]{1,0:T(8,128)(2,1)} fusion(bf16[4096,512]{1,0:T(8,128)(2,1)S(1)} %copy-done.4, f32[512,1792]{1,0:T(8,128)S(1)} %fusion), kind=kOutput, calls=%fused_computation | convolution fusion | flops 7531790336 | bytes 22544384 | tf_op jit(solution)/shard_map/dot_general | solution.py:133
  453.1 0.1 dynamic-slice_bitcast_fusion
  453.3 1.7 copy.6
  (4 shorter events, 0.0 us)
Async XLA Ops:
  7.2 88.7 %reduce-scatter.3.cloned.1.call-start = ((), (), s32[]{:S(2)}) async-start(), calls=%async_computation.2 | async-start | bytes 2228224 | tf_op jit(solution)/shard_map/reduce_scatter | solution.py:92
  20.4 5.5 %copy-start.2 = (bf16[4096,1792]{1,0:T(8,128)(2,1)}, bf16[4096,1792]{1,0:T(8,128)(2,1)S(1)}, u32[]{:S(2)}) copy-start(bf16[4096,1792]{1,0:T(8,128)(2,1)S(1)} %add_convert_fusion) | copy-start | bytes 44040196
  31.2 129.8 %reduce-scatter.5.cloned.1.call-start = ((), (), s32[]{:S(2)}) async-start(), calls=%async_computation.3 | async-start | bytes 2228224 | tf_op jit(solution)/shard_map/reduce_scatter | solution.py:92
  31.3 23.4 %collective-permute-start = (bf16[1792,256]{1,0:T(8,128)(2,1)S(1)}, bf16[1792,256]{1,0:T(8,128)(2,1)S(1)}, u32[]{:S(2)}, u32[]{:S(2)}) collective-permute-start(bf16[1792,256]{1,0:T(8,128)(2,1)S(1)} %convert_element_type.58), channel_id=1, source_target_pairs={{0,16},{16,0},{1,17},{17,1},{2,18},{18,2},{3,19},{19,3},{4,20},{20... | collective-permute-start | bytes 2752520 | tf_op jit(solution)/shard_map/ppermute | solution.py:95
  65.2 231.2 %all-reduce.2.cloned.1.call-start = ((), (), s32[]{:S(2)}) async-start(), calls=%async_computation.5 | async-start | bytes 2097152 | tf_op jit(solution)/shard_map/psum | solution.py:106
  162.2 1.6 copy-start.6
  163.5 185.9 %all-gather.2.cloned.1.call-start = ((), (), s32[]{:S(2)}) async-start(), calls=%async_computation.4 | async-start | bytes 4456448 | tf_op jit(solution)/shard_map/all_gather | solution.py:110
  296.4 1.2 copy-start
  349.4 4.9 %copy-start.1 = (bf16[4096,512]{1,0:T(8,128)(2,1)S(1)}, bf16[4096,512]{1,0:T(8,128)(2,1)}, u32[]{:S(2)}) copy-start(bf16[4096,512]{1,0:T(8,128)(2,1)} %all-gather.2.cloned.1.call-done) | copy-start | bytes 12582916
  356.8 13.8 %copy-start.3 = (bf16[4096,512]{1,0:T(8,128)(2,1)}, bf16[4096,512]{1,0:T(8,128)(2,1)S(1)}, u32[]{:S(2)}) copy-start(bf16[4096,512]{1,0:T(8,128)(2,1)S(1)} %add_convert_fusion.1) | copy-start | bytes 12582916
  370.6 41.5 %collective-permute-start.1 = (bf16[512,1792]{1,0:T(8,128)(2,1)S(1)}, bf16[512,1792]{1,0:T(8,128)(2,1)S(1)}, u32[]{:S(2)}, u32[]{:S(2)}) collective-permute-start(bf16[512,1792]{1,0:T(8,128)(2,1)S(1)} %convolution_convert_fusion.2), channel_id=1, source_target_pairs={{0,16},{16,0},{1,17},{17,1},{2,18},{18,2},{3,19},{19,3},{4,20},{20... | collective-permute-start | bytes 5505032 | tf_op jit(solution)/shard_map/ppermute | solution.py:124
  412.1 1.2 copy-start.5
  414.0 1.2 collective-permute-start.2
  415.2 3.6 collective-permute-start.3
  418.8 3.6 collective-permute-start.4
  422.4 17.4 %collective-permute-start.5 = (f32[512]{0:T(512)S(1)}, f32[512]{0:T(512)S(1)}, u32[]{:S(2)}, u32[]{:S(2)}) collective-permute-start(f32[512]{0:T(512)S(1)} %add.41), channel_id=1, source_target_pairs={{0,8},{1,9},{2,10},{3,11},{4,12},{5,13},{6,14},{7,15},{8,0},{9,1},... | collective-permute-start | bytes 6152 | tf_op jit(solution)/shard_map/ppermute | solution.py:74
  439.9 2.7 copy-start.4
Sparse Core Ops, SparseCore 0:
  31.3 64.5 reduce-scatter.2
  100.2 60.7 reduce-scatter.4
  166.8 129.5 all-reduce.1
  299.0 49.6 all-gather.1
